TPU v7x, 32 devices: a whole 2x2x4 slice. The times are simulated.
32 devices in a mesh: data: 2 (over x), dap2: 4 (over z), dap: 4 (over y, core).
Axes of the slice: x: 2, y: 2, z: 4, core: 2. Of those that a mesh axis runs over, the one named last changes fastest.
Arguments:
- pair_rep: bfloat16 [512, 256, 128], P(('data', 'dap2', 'dap')), parts along dimension 0
- pair_mask: int32 [512, 256], P(('data', 'dap2', 'dap')), parts along dimension 0
- norm_in: bfloat16 [16, 2, 2, 128], replicated
- norm_out: bfloat16 [16, 2, 2, 128], replicated
- w_ab: bfloat16 [16, 2, 128, 512], replicated
- w_gate: bfloat16 [16, 2, 128, 128], replicated
- w_out: bfloat16 [16, 2, 128, 128], replicated
Outputs:
- output: bfloat16 [512, 256, 128], P(('data', 'dap2', 'dap')), parts along dimension 0
There are 2 independent parts. A program takes and returns all parts, laid end to end along the dimension named above; an argument that names none is the same for every part.
All inputs are finite; a program needn't handle non-finite values.
Results may differ from a plain program's by a relative error of at most 0.02.
Values are sent between devices in bfloat16 or wider.
A program may use at most 1 GiB of HBM per device.

v0:
```python
import jax
import jax.numpy as jnp
from jax import lax
from jax.sharding import PartitionSpec as P

LN_EPS = 1e-5
ROW_AXES = ("dap2", "dap")
ALL_ROWS = ("data", "dap2", "dap")


def layer_norm(values, gain_vec, shift_vec, norm_axis):
    mean_val = jnp.mean(values, axis=norm_axis, keepdims=True)
    centered = values - mean_val
    var_val = jnp.mean(centered * centered, axis=norm_axis, keepdims=True)
    return centered * lax.rsqrt(var_val + LN_EPS) * gain_vec + shift_vec


def row_inputs(pair_loc, mask_loc, norm_in, w_ab):
    hidden = w_ab.shape[1] // 4
    pair_f = pair_loc.astype(jnp.float32)
    x_ln = layer_norm(pair_f, norm_in[0].astype(jnp.float32), norm_in[1].astype(jnp.float32), -1).astype(jnp.bfloat16)
    proj_all = jnp.einsum("de,ikd->eik", w_ab, x_ln, preferred_element_type=jnp.float32)
    proj_four = proj_all.reshape(2, 2, hidden, pair_loc.shape[0], pair_loc.shape[1])
    ab_rows = (mask_loc * jax.nn.sigmoid(proj_four[:, 1]) * proj_four[:, 0]).astype(jnp.bfloat16)
    return pair_f, x_ln, ab_rows


def finish_update(pair_f, x_ln, tri_rows, norm_out, w_gate, w_out):
    gain_vec = norm_out[0].astype(jnp.float32)[:, None, None]
    shift_vec = norm_out[1].astype(jnp.float32)[:, None, None]
    y_ln = layer_norm(tri_rows.astype(jnp.float32), gain_vec, shift_vec, 0).astype(jnp.bfloat16)
    update_val = jnp.einsum("cij,cd->ijd", y_ln, w_out, preferred_element_type=jnp.float32)
    gate_val = jax.nn.sigmoid(jnp.einsum("ijd,de->ije", x_ln, w_gate, preferred_element_type=jnp.float32))
    return (pair_f + gate_val * update_val).astype(jnp.bfloat16)


def tri_update(pair_loc, mask_loc, norm_in, norm_out, w_ab, w_gate, w_out, outgoing):
    pair_f, x_ln, ab_rows = row_inputs(pair_loc, mask_loc, norm_in, w_ab)
    ab_cols = lax.all_to_all(ab_rows, ROW_AXES, 1, 2, tiled=True)
    einsum_form = "cik,cjk->cij" if outgoing else "cki,ckj->cij"
    tri_full = jnp.einsum(einsum_form, ab_cols[0], ab_cols[1], preferred_element_type=jnp.float32).astype(jnp.bfloat16)
    tri_rows = lax.all_to_all(tri_full, ROW_AXES, 1, 0, tiled=True)
    return finish_update(pair_f, x_ln, tri_rows, norm_out, w_gate, w_out)


def solution(mesh):
    row_spec = P(ALL_ROWS, None, None)
    mask_spec = P(ALL_ROWS, None)

    def local_stack(pair_rep, pair_mask, norm_in, norm_out, w_ab, w_gate, w_out):
        mask_f = pair_mask.astype(jnp.float32)
        pair_cur = pair_rep
        for layer_idx in range(w_ab.shape[0]):
            for upd_idx in range(2):
                pair_cur = tri_update(pair_cur, mask_f, norm_in[layer_idx, upd_idx], norm_out[layer_idx, upd_idx], w_ab[layer_idx, upd_idx], w_gate[layer_idx, upd_idx], w_out[layer_idx, upd_idx], upd_idx == 0)
        return pair_cur

    return jax.shard_map(local_stack, mesh=mesh, in_specs=(row_spec, mask_spec, P(), P(), P(), P(), P()), out_specs=row_spec, check_vma=False)
```

profile of v0, /device:TPU:0, one launch (start us, length us, event | category | flops | bytes accessed | tf_op | source)
XLA Modules:
  0.0 4323.3 jit_solution(15329002574592125151)
XLA Ops:
  48.9 55.1 %all_to_all.768 = bf16[2,128,16,256]{3,2,0,1:T(8,128)(2,1)S(1)} all-to-all(bf16[2,128,16,256]{3,2,0,1:T(8,128)(2,1)S(1)} %fusion.31), channel_id=1, replica_groups=mesh['data'=2,'dap2'=4,'dap'=4] {'dap2','dap'}, dimensions={1} | all-to-all | bytes 4194304 | tf_op jit(solution)/shard_map/all_to_all | solution.py:39
  115.0 18.7 all-to-all-done.1
  184.5 54.7 %all_to_all.769 = bf16[2,128,16,256]{3,2,0,1:T(8,128)(2,1)S(1)} all-to-all(bf16[2,128,16,256]{3,2,0,1:T(8,128)(2,1)S(1)} %fusion.30), channel_id=1, replica_groups=mesh['data'=2,'dap2'=4,'dap'=4] {'dap2','dap'}, dimensions={1} | all-to-all | bytes 4194304 | tf_op jit(solution)/shard_map/all_to_all | solution.py:39
  249.0 19.5 all-to-all-done.3
  319.4 54.7 %all_to_all.770 = bf16[2,128,16,256]{3,2,0,1:T(8,128)(2,1)S(1)} all-to-all(bf16[2,128,16,256]{3,2,0,1:T(8,128)(2,1)S(1)} %fusion.29), channel_id=1, replica_groups=mesh['data'=2,'dap2'=4,'dap'=4] {'dap2','dap'}, dimensions={1} | all-to-all | bytes 4194304 | tf_op jit(solution)/shard_map/all_to_all | solution.py:39
  384.5 18.9 all-to-all-done.5
  454.2 54.7 %all_to_all.771 = bf16[2,128,16,256]{3,2,0,1:T(8,128)(2,1)S(1)} all-to-all(bf16[2,128,16,256]{3,2,0,1:T(8,128)(2,1)S(1)} %fusion.28), channel_id=1, replica_groups=mesh['data'=2,'dap2'=4,'dap'=4] {'dap2','dap'}, dimensions={1} | all-to-all | bytes 4194304 | tf_op jit(solution)/shard_map/all_to_all | solution.py:39
  519.0 19.5 all-to-all-done.7
  589.3 54.7 %all_to_all.772 = bf16[2,128,16,256]{3,2,0,1:T(8,128)(2,1)S(1)} all-to-all(bf16[2,128,16,256]{3,2,0,1:T(8,128)(2,1)S(1)} %fusion.27), channel_id=1, replica_groups=mesh['data'=2,'dap2'=4,'dap'=4] {'dap2','dap'}, dimensions={1} | all-to-all | bytes 4194304 | tf_op jit(solution)/shard_map/all_to_all | solution.py:39
  653.9 19.5 all-to-all-done.9
  724.2 54.7 %all_to_all.773 = bf16[2,128,16,256]{3,2,0,1:T(8,128)(2,1)S(1)} all-to-all(bf16[2,128,16,256]{3,2,0,1:T(8,128)(2,1)S(1)} %fusion.26), channel_id=1, replica_groups=mesh['data'=2,'dap2'=4,'dap'=4] {'dap2','dap'}, dimensions={1} | all-to-all | bytes 4194304 | tf_op jit(solution)/shard_map/all_to_all | solution.py:39
  789.4 18.9 all-to-all-done.11
  859.1 54.7 %all_to_all.774 = bf16[2,128,16,256]{3,2,0,1:T(8,128)(2,1)S(1)} all-to-all(bf16[2,128,16,256]{3,2,0,1:T(8,128)(2,1)S(1)} %fusion.25), channel_id=1, replica_groups=mesh['data'=2,'dap2'=4,'dap'=4] {'dap2','dap'}, dimensions={1} | all-to-all | bytes 4194304 | tf_op jit(solution)/shard_map/all_to_all | solution.py:39
  923.8 19.5 all-to-all-done.13
  994.2 54.7 %all_to_all.775 = bf16[2,128,16,256]{3,2,0,1:T(8,128)(2,1)S(1)} all-to-all(bf16[2,128,16,256]{3,2,0,1:T(8,128)(2,1)S(1)} %fusion.24), channel_id=1, replica_groups=mesh['data'=2,'dap2'=4,'dap'=4] {'dap2','dap'}, dimensions={1} | all-to-all | bytes 4194304 | tf_op jit(solution)/shard_map/all_to_all | solution.py:39
  1058.7 19.5 all-to-all-done.15
  1129.0 54.7 %all_to_all.776 = bf16[2,128,16,256]{3,2,0,1:T(8,128)(2,1)S(1)} all-to-all(bf16[2,128,16,256]{3,2,0,1:T(8,128)(2,1)S(1)} %fusion.23), channel_id=1, replica_groups=mesh['data'=2,'dap2'=4,'dap'=4] {'dap2','dap'}, dimensions={1} | all-to-all | bytes 4194304 | tf_op jit(solution)/shard_map/all_to_all | solution.py:39
  1193.6 19.5 all-to-all-done.17
  1263.9 54.7 %all_to_all.777 = bf16[2,128,16,256]{3,2,0,1:T(8,128)(2,1)S(1)} all-to-all(bf16[2,128,16,256]{3,2,0,1:T(8,128)(2,1)S(1)} %fusion.22), channel_id=1, replica_groups=mesh['data'=2,'dap2'=4,'dap'=4] {'dap2','dap'}, dimensions={1} | all-to-all | bytes 4194304 | tf_op jit(solution)/shard_map/all_to_all | solution.py:39
  1328.7 19.5 all-to-all-done.19
  1399.0 54.7 %all_to_all.778 = bf16[2,128,16,256]{3,2,0,1:T(8,128)(2,1)S(1)} all-to-all(bf16[2,128,16,256]{3,2,0,1:T(8,128)(2,1)S(1)} %fusion.21), channel_id=1, replica_groups=mesh['data'=2,'dap2'=4,'dap'=4] {'dap2','dap'}, dimensions={1} | all-to-all | bytes 4194304 | tf_op jit(solution)/shard_map/all_to_all | solution.py:39
  1463.6 19.5 all-to-all-done.21
  1533.9 54.7 %all_to_all.779 = bf16[2,128,16,256]{3,2,0,1:T(8,128)(2,1)S(1)} all-to-all(bf16[2,128,16,256]{3,2,0,1:T(8,128)(2,1)S(1)} %fusion.20), channel_id=1, replica_groups=mesh['data'=2,'dap2'=4,'dap'=4] {'dap2','dap'}, dimensions={1} | all-to-all | bytes 4194304 | tf_op jit(solution)/shard_map/all_to_all | solution.py:39
  1598.6 19.5 all-to-all-done.23
  1668.9 54.7 %all_to_all.780 = bf16[2,128,16,256]{3,2,0,1:T(8,128)(2,1)S(1)} all-to-all(bf16[2,128,16,256]{3,2,0,1:T(8,128)(2,1)S(1)} %fusion.19), channel_id=1, replica_groups=mesh['data'=2,'dap2'=4,'dap'=4] {'dap2','dap'}, dimensions={1} | all-to-all | bytes 4194304 | tf_op jit(solution)/shard_map/all_to_all | solution.py:39
  1734.3 18.9 all-to-all-done.25
  1804.0 54.7 %all_to_all.781 = bf16[2,128,16,256]{3,2,0,1:T(8,128)(2,1)S(1)} all-to-all(bf16[2,128,16,256]{3,2,0,1:T(8,128)(2,1)S(1)} %fusion.18), channel_id=1, replica_groups=mesh['data'=2,'dap2'=4,'dap'=4] {'dap2','dap'}, dimensions={1} | all-to-all | bytes 4194304 | tf_op jit(solution)/shard_map/all_to_all | solution.py:39
  1868.6 19.5 all-to-all-done.27
  1938.9 54.7 %all_to_all.782 = bf16[2,128,16,256]{3,2,0,1:T(8,128)(2,1)S(1)} all-to-all(bf16[2,128,16,256]{3,2,0,1:T(8,128)(2,1)S(1)} %fusion.17), channel_id=1, replica_groups=mesh['data'=2,'dap2'=4,'dap'=4] {'dap2','dap'}, dimensions={1} | all-to-all | bytes 4194304 | tf_op jit(solution)/shard_map/all_to_all | solution.py:39
  2004.1 18.9 all-to-all-done.29
  2073.8 54.7 %all_to_all.783 = bf16[2,128,16,256]{3,2,0,1:T(8,128)(2,1)S(1)} all-to-all(bf16[2,128,16,256]{3,2,0,1:T(8,128)(2,1)S(1)} %fusion.16), channel_id=1, replica_groups=mesh['data'=2,'dap2'=4,'dap'=4] {'dap2','dap'}, dimensions={1} | all-to-all | bytes 4194304 | tf_op jit(solution)/shard_map/all_to_all | solution.py:39
  2138.5 19.5 all-to-all-done.31
  2208.9 54.7 %all_to_all.784 = bf16[2,128,16,256]{3,2,0,1:T(8,128)(2,1)S(1)} all-to-all(bf16[2,128,16,256]{3,2,0,1:T(8,128)(2,1)S(1)} %fusion.15), channel_id=1, replica_groups=mesh['data'=2,'dap2'=4,'dap'=4] {'dap2','dap'}, dimensions={1} | all-to-all | bytes 4194304 | tf_op jit(solution)/shard_map/all_to_all | solution.py:39
  2273.4 19.5 all-to-all-done.33
  2343.7 54.7 %all_to_all.785 = bf16[2,128,16,256]{3,2,0,1:T(8,128)(2,1)S(1)} all-to-all(bf16[2,128,16,256]{3,2,0,1:T(8,128)(2,1)S(1)} %fusion.14), channel_id=1, replica_groups=mesh['data'=2,'dap2'=4,'dap'=4] {'dap2','dap'}, dimensions={1} | all-to-all | bytes 4194304 | tf_op jit(solution)/shard_map/all_to_all | solution.py:39
  2408.3 19.5 all-to-all-done.35
  2478.6 54.7 %all_to_all.786 = bf16[2,128,16,256]{3,2,0,1:T(8,128)(2,1)S(1)} all-to-all(bf16[2,128,16,256]{3,2,0,1:T(8,128)(2,1)S(1)} %fusion.13), channel_id=1, replica_groups=mesh['data'=2,'dap2'=4,'dap'=4] {'dap2','dap'}, dimensions={1} | all-to-all | bytes 4194304 | tf_op jit(solution)/shard_map/all_to_all | solution.py:39
  2543.4 19.5 all-to-all-done.37
  2613.7 54.7 %all_to_all.787 = bf16[2,128,16,256]{3,2,0,1:T(8,128)(2,1)S(1)} all-to-all(bf16[2,128,16,256]{3,2,0,1:T(8,128)(2,1)S(1)} %fusion.12), channel_id=1, replica_groups=mesh['data'=2,'dap2'=4,'dap'=4] {'dap2','dap'}, dimensions={1} | all-to-all | bytes 4194304 | tf_op jit(solution)/shard_map/all_to_all | solution.py:39
  2678.3 19.5 all-to-all-done.39
  2748.6 54.7 %all_to_all.788 = bf16[2,128,16,256]{3,2,0,1:T(8,128)(2,1)S(1)} all-to-all(bf16[2,128,16,256]{3,2,0,1:T(8,128)(2,1)S(1)} %fusion.11), channel_id=1, replica_groups=mesh['data'=2,'dap2'=4,'dap'=4] {'dap2','dap'}, dimensions={1} | all-to-all | bytes 4194304 | tf_op jit(solution)/shard_map/all_to_all | solution.py:39
  2813.2 19.5 all-to-all-done.41
  2883.6 54.7 %all_to_all.789 = bf16[2,128,16,256]{3,2,0,1:T(8,128)(2,1)S(1)} all-to-all(bf16[2,128,16,256]{3,2,0,1:T(8,128)(2,1)S(1)} %fusion.10), channel_id=1, replica_groups=mesh['data'=2,'dap2'=4,'dap'=4] {'dap2','dap'}, dimensions={1} | all-to-all | bytes 4194304 | tf_op jit(solution)/shard_map/all_to_all | solution.py:39
  2949.0 18.9 all-to-all-done.43
  3018.7 54.7 %all_to_all.790 = bf16[2,128,16,256]{3,2,0,1:T(8,128)(2,1)S(1)} all-to-all(bf16[2,128,16,256]{3,2,0,1:T(8,128)(2,1)S(1)} %fusion.9), channel_id=1, replica_groups=mesh['data'=2,'dap2'=4,'dap'=4] {'dap2','dap'}, dimensions={1} | all-to-all | bytes 4194304 | tf_op jit(solution)/shard_map/all_to_all | solution.py:39
  3083.9 18.9 all-to-all-done.45
  3153.5 54.7 %all_to_all.791 = bf16[2,128,16,256]{3,2,0,1:T(8,128)(2,1)S(1)} all-to-all(bf16[2,128,16,256]{3,2,0,1:T(8,128)(2,1)S(1)} %fusion.8), channel_id=1, replica_groups=mesh['data'=2,'dap2'=4,'dap'=4] {'dap2','dap'}, dimensions={1} | all-to-all | bytes 4194304 | tf_op jit(solution)/shard_map/all_to_all | solution.py:39
  3218.1 19.5 all-to-all-done.47
  3288.4 54.7 %all_to_all.792 = bf16[2,128,16,256]{3,2,0,1:T(8,128)(2,1)S(1)} all-to-all(bf16[2,128,16,256]{3,2,0,1:T(8,128)(2,1)S(1)} %fusion.7), channel_id=1, replica_groups=mesh['data'=2,'dap2'=4,'dap'=4] {'dap2','dap'}, dimensions={1} | all-to-all | bytes 4194304 | tf_op jit(solution)/shard_map/all_to_all | solution.py:39
  3353.2 19.5 all-to-all-done.49
  3423.5 54.7 %all_to_all.793 = bf16[2,128,16,256]{3,2,0,1:T(8,128)(2,1)S(1)} all-to-all(bf16[2,128,16,256]{3,2,0,1:T(8,128)(2,1)S(1)} %fusion.6), channel_id=1, replica_groups=mesh['data'=2,'dap2'=4,'dap'=4] {'dap2','dap'}, dimensions={1} | all-to-all | bytes 4194304 | tf_op jit(solution)/shard_map/all_to_all | solution.py:39
  3488.0 19.5 all-to-all-done.51
  3558.4 54.7 %all_to_all.794 = bf16[2,128,16,256]{3,2,0,1:T(8,128)(2,1)S(1)} all-to-all(bf16[2,128,16,256]{3,2,0,1:T(8,128)(2,1)S(1)} %fusion.5), channel_id=1, replica_groups=mesh['data'=2,'dap2'=4,'dap'=4] {'dap2','dap'}, dimensions={1} | all-to-all | bytes 4194304 | tf_op jit(solution)/shard_map/all_to_all | solution.py:39
  3622.9 19.5 all-to-all-done.53
  3693.3 54.7 %all_to_all.795 = bf16[2,128,16,256]{3,2,0,1:T(8,128)(2,1)S(1)} all-to-all(bf16[2,128,16,256]{3,2,0,1:T(8,128)(2,1)S(1)} %fusion.4), channel_id=1, replica_groups=mesh['data'=2,'dap2'=4,'dap'=4] {'dap2','dap'}, dimensions={1} | all-to-all | bytes 4194304 | tf_op jit(solution)/shard_map/all_to_all | solution.py:39
  3758.1 19.5 all-to-all-done.55
  3828.4 54.7 %all_to_all.796 = bf16[2,128,16,256]{3,2,0,1:T(8,128)(2,1)S(1)} all-to-all(bf16[2,128,16,256]{3,2,0,1:T(8,128)(2,1)S(1)} %fusion.3), channel_id=1, replica_groups=mesh['data'=2,'dap2'=4,'dap'=4] {'dap2','dap'}, dimensions={1} | all-to-all | bytes 4194304 | tf_op jit(solution)/shard_map/all_to_all | solution.py:39
  3892.9 19.5 all-to-all-done.57
  3963.3 54.7 %all_to_all.797 = bf16[2,128,16,256]{3,2,0,1:T(8,128)(2,1)S(1)} all-to-all(bf16[2,128,16,256]{3,2,0,1:T(8,128)(2,1)S(1)} %fusion.2), channel_id=1, replica_groups=mesh['data'=2,'dap2'=4,'dap'=4] {'dap2','dap'}, dimensions={1} | all-to-all | bytes 4194304 | tf_op jit(solution)/shard_map/all_to_all | solution.py:39
  4027.9 19.5 all-to-all-done.59
  4098.2 54.7 %all_to_all.798 = bf16[2,128,16,256]{3,2,0,1:T(8,128)(2,1)S(1)} all-to-all(bf16[2,128,16,256]{3,2,0,1:T(8,128)(2,1)S(1)} %fusion.1), channel_id=1, replica_groups=mesh['data'=2,'dap2'=4,'dap'=4] {'dap2','dap'}, dimensions={1} | all-to-all | bytes 4194304 | tf_op jit(solution)/shard_map/all_to_all | solution.py:39
  4162.8 19.5 all-to-all-done.61
  4233.2 54.7 %all_to_all.799 = bf16[2,128,16,256]{3,2,0,1:T(8,128)(2,1)S(1)} all-to-all(bf16[2,128,16,256]{3,2,0,1:T(8,128)(2,1)S(1)} %fusion), channel_id=1, replica_groups=mesh['data'=2,'dap2'=4,'dap'=4] {'dap2','dap'}, dimensions={1} | all-to-all | bytes 4194304 | tf_op jit(solution)/shard_map/all_to_all | solution.py:39
  4298.0 19.4 all-to-all-done.63
  (969 shorter events, 1946.9 us)
Async XLA Ops:
  36.9 7.4 copy-start.38
  106.6 27.1 all-to-all-start.1
  241.8 26.8 all-to-all-start.3
  376.6 26.8 all-to-all-start.5
  511.5 27.0 all-to-all-start.7
  646.6 26.8 all-to-all-start.9
  779.9 6.0 copy-start.35
  781.5 26.8 all-to-all-start.11
  916.4 27.0 all-to-all-start.13
  1051.5 26.8 all-to-all-start.15
  1186.3 26.8 all-to-all-start.17
  1321.2 27.0 all-to-all-start.19
  1454.8 5.9 copy-start.88
  1454.8 6.0 copy-start.86
  1456.3 26.8 all-to-all-start.21
  1484.7 2.3 copy-start.46
  1589.7 6.0 copy-start.82
  1589.7 6.1 copy-start.80
  1591.3 26.8 all-to-all-start.23
  1724.6 6.2 copy-start.75
  1724.6 6.3 copy-start.74
  1724.6 6.3 copy-start.33
  1726.2 27.0 all-to-all-start.25
  1859.7 5.9 copy-start.70
  1859.8 6.0 copy-start.69
  1861.3 26.8 all-to-all-start.27
  1994.6 6.0 copy-start.36
  1996.2 26.8 all-to-all-start.29
  2131.1 27.0 all-to-all-start.31
  2266.1 26.8 all-to-all-start.33
  2401.0 26.8 all-to-all-start.35
  2535.9 27.0 all-to-all-start.37
  2669.4 5.9 copy-start.89
  2669.5 6.0 copy-start.87
  2671.0 26.8 all-to-all-start.39
  2804.4 6.0 copy-start.83
  2804.4 6.1 copy-start.81
  2805.9 26.8 all-to-all-start.41
  2939.3 6.2 copy-start.77
  2939.3 6.3 copy-start.76
  2939.3 6.3 copy-start.34
  2940.9 27.0 all-to-all-start.43
  3074.4 5.9 copy-start.71
  3074.4 6.0 copy-start.37
  3076.0 26.8 all-to-all-start.45
  3210.8 26.8 all-to-all-start.47
  3345.7 27.0 all-to-all-start.49
  3480.8 26.8 all-to-all-start.51
  3615.6 26.8 all-to-all-start.53
  3749.0 6.2 copy-start.91
  3749.0 6.2 copy-start.90
  3750.6 27.0 all-to-all-start.55
  3884.1 5.9 copy-start.85
  3884.1 6.0 copy-start.84
  3885.7 26.8 all-to-all-start.57
  4019.0 6.0 copy-start.79
  4019.0 6.1 copy-start.78
  4020.6 26.8 all-to-all-start.59
  4153.9 6.0 copy-start.73
  4153.9 6.1 copy-start.72
  4155.5 26.9 all-to-all-start.61
  4288.9 6.1 copy-start.68
  4288.9 6.2 copy-start.67
  4290.5 26.9 all-to-all-start.63
  (60 other events, 115.5 us)
where the time goes:
time: 4360 us; the launch traced here: 4320 us
  blocking collectives  1750 us (40%)
  local copies, waits for them, and re-layouts  1280 us (29%)
  waiting for transfers between devices  620 us (14%)
  matrix products  342 us (8%)
  other arithmetic  182 us (4%)
  starting transfers between devices  142 us (3%)
    all_to_all x32, blocking collectives, tri_update(): ab_cols = lax.all_to_all(ab_rows, ROW_AXES, 1, 2, tiled=True)  1750 us
    all_to_all x32, waiting for transfers between devices, tri_update(): tri_rows = lax.all_to_all(tri_full, ROW_AXES, 1, 0, tiled=True)  620 us
    unnamed x249, local copies, waits for them, and re-layouts  506 us
    slice x32, local copies, waits for them, and re-layouts, row_inputs(): proj_four[:, 1]  366 us
    reshape x32, local copies, waits for them, and re-layouts, row_inputs(): proj_all.reshape(2, 2, hidden, pair_loc.shape[0], pair_loc.shape[1])  337 us
    dot_general x32, matrix products, row_inputs(): jnp.einsum('de,ikd->eik', w_ab, x_ln, preferred_element_type=jnp.float32)  177 us
    convert_element_type x32, other arithmetic, row_inputs(): (mask_loc * jax.nn.sigmoid(proj_four[:, 1]) * proj_four[:, 0]).astype(jnp...  151 us
    all_to_all x32, starting transfers between devices, tri_update(): tri_rows = lax.all_to_all(tri_full, ROW_AXES, 1, 0, tiled=True)  142 us
  transfers between devices with their start and end apart: 32, of which 32 were waited for; matrix products, arithmetic and copies ran while one was open for 2% of the time, Pallas kernels for 0%

commit v1 on v0

v1 whole, which is shorter than its diff:
```python
import functools

import jax
import jax.numpy as jnp
from jax import lax
from jax.experimental import pallas as pl
from jax.experimental.pallas import tpu as pltpu
from jax.sharding import PartitionSpec as P

LN_EPS = 1e-5
ALL_ROWS = ("data", "dap2", "dap")
MESH = pl.DeviceIdType.MESH
F32, BF16 = jnp.float32, jnp.bfloat16
C = 128
CO = C // 2
LANES = 128
Y_PITCH = 132


def layer_norm(v, gain, shift):
    centered = v - jnp.sum(v, axis=0, keepdims=True) * (1.0 / C)
    var = jnp.sum(centered * centered, axis=0, keepdims=True) * (1.0 / C)
    return (centered * lax.rsqrt(var + LN_EPS) * gain + shift).astype(BF16)


def dot(lhs, rhs, dims=((1,), (0,))):
    return lax.dot_general(lhs, rhs, (dims, ((), ())), preferred_element_type=F32)


def kernel(nz, ny, n_upd, z_in, m_in, w_in, n_in, out, z_ref, x_ref, ab_ref, t_ref, ts_ref, abs_ref, s_ref, y_ref,
           m_ref, w_ref, n_ref, in_sem, w_sem, zsend, zrecv, msend, mrecv, ab_send, ab_recv, t_send, t_recv):
    G = z_in.shape[0]
    NR = z_ref.shape[0]
    NG = NR // G
    N = 2 * NR
    ST = s_ref.shape[1] // (2 * C)
    zi = lax.axis_index("dap2")
    dap = lax.axis_index("dap")
    yi, side = dap // 2, dap % 2
    q = zi * ny + yi
    partner = {"dap": yi * 2 + 1 - side}
    ypeer = {"dap": (1 - yi) * 2 + side}
    up, down = {"dap2": zi + 1}, {"dap2": zi - 1}
    mine = pl.multiple_of(side * NR, NR)

    barrier = pltpu.get_barrier_semaphore()
    pl.semaphore_signal(barrier, inc=1, device_id=partner, device_id_type=MESH)
    if ny > 1:
        pl.semaphore_signal(barrier, inc=1, device_id=ypeer, device_id_type=MESH)

    @pl.when(zi < nz - 1)
    def _():
        pl.semaphore_signal(barrier, inc=1, device_id=up, device_id_type=MESH)

    @pl.when(zi > 0)
    def _():
        pl.semaphore_signal(barrier, inc=1, device_id=down, device_id_type=MESH)

    def params(s):
        slot = s % 2
        return (
            pltpu.make_async_copy(w_in.at[s], w_ref.at[slot], w_sem.at[slot, 0]),
            pltpu.make_async_copy(n_in.at[s], n_ref.at[slot], w_sem.at[slot, 1]),
        )

    for s in range(2):
        for cp in params(s):
            cp.start()

    def rows_of(block):
        return pl.ds(pl.multiple_of(block * G, G), G)

    loads = (
        pltpu.make_async_copy(z_in, z_ref.at[rows_of(q)], in_sem.at[0]),
        pltpu.make_async_copy(m_in, m_ref.at[:, rows_of(q)], in_sem.at[1]),
    )
    for cp in loads:
        cp.start()
    for cp in loads:
        cp.wait()

    neighbours = (2 if ny > 1 else 1) + jnp.where(zi < nz - 1, 1, 0) + jnp.where(zi > 0, 1, 0)
    pl.semaphore_wait(barrier, neighbours)

    def block_copies(block, to, k):
        rows = rows_of(block)
        return (
            pltpu.make_async_remote_copy(z_ref.at[rows], z_ref.at[rows], zsend.at[k], zrecv.at[k], device_id=to, device_id_type=MESH),
            pltpu.make_async_remote_copy(m_ref.at[:, rows], m_ref.at[:, rows], msend.at[k], mrecv.at[k], device_id=to, device_id_type=MESH),
        )

    K_DOWN, K_Y = nz - 1, 2 * (nz - 1)

    def start(copies):
        for cp in copies:
            cp.start()

    def gather(step):
        d = step
        if d == 0:
            if ny > 1:
                start(block_copies(q, ypeer, K_Y + zi))
        have_low, have_high = zi - d >= 0, zi + d <= nz - 1
        low, high = (zi - d) * ny + yi, (zi + d) * ny + yi
        if d > 0:
            @pl.when(have_low)
            def _():
                for cp in block_copies(low, up, d - 1):
                    cp.wait_recv()
                if ny > 1:
                    start(block_copies(low, ypeer, K_Y + zi - d))

            @pl.when(have_high)
            def _():
                for cp in block_copies(high, down, K_DOWN + d - 1):
                    cp.wait_recv()
                if ny > 1:
                    start(block_copies(high, ypeer, K_Y + zi + d))
        if d < nz - 1:
            @pl.when(jnp.logical_and(have_low, zi < nz - 1))
            def _():
                start(block_copies(low, up, d))

            @pl.when(jnp.logical_and(have_high, zi > 0))
            def _():
                start(block_copies(high, down, K_DOWN + d))

    for d in range(nz):
        gather(d)
    if ny > 1:
        for zz in range(nz):
            for cp in block_copies(zz * ny + 1 - yi, ypeer, K_Y + zz):
                cp.wait_recv()
    for d in range(nz - 1):
        @pl.when(jnp.logical_and(zi - d >= 0, zi < nz - 1))
        def _():
            for cp in block_copies((zi - d) * ny + yi, up, d):
                cp.wait_send()

        @pl.when(jnp.logical_and(zi + d <= nz - 1, zi > 0))
        def _():
            for cp in block_copies((zi + d) * ny + yi, down, K_DOWN + d):
                cp.wait_send()
    if ny > 1:
        for zz in range(nz):
            for cp in block_copies(zz * ny + yi, ypeer, K_Y + zz):
                cp.wait_send()

    def swap_t(g):
        @pl.loop(0, C, step=16)
        def _(c0):
            for dc in range(16):
                for h in range(2):
                    v = t_ref[c0 + dc, h, rows_of(g), :].astype(F32)
                    y_ref[h, pl.ds(c0 + dc, G, stride=Y_PITCH), :] = v

    def finish_row(g, r, slot):
        row = g * G + r
        y = [layer_norm(y_ref[h, pl.ds(r * Y_PITCH, C), :], n_ref[slot, 2], n_ref[slot, 3]) for h in range(2)]
        upd = dot(w_ref[slot, 5 * C:6 * C, :], jnp.concatenate(y, axis=1))
        gate = dot(w_ref[slot, 4 * C:5 * C, :], jnp.concatenate([x_ref[row, 0], x_ref[row, 1]], axis=1))
        z_new = []
        for h in range(2):
            ls = slice(h * LANES, (h + 1) * LANES)
            zn = (z_ref[row, h].astype(F32) + (jnp.tanh(gate[:, ls]) + 1.0) * upd[:, ls]).astype(BF16)
            z_ref[row, h] = zn
            z_new.append(zn)
        return z_new

    def start_row(g, r, slot, z_row):
        row = g * G + r
        xm = []
        for h in range(2):
            x = layer_norm(z_row[h].astype(F32), n_ref[slot, 0], n_ref[slot, 1])
            x_ref[row, h] = x
            mask = jnp.broadcast_to(m_ref[h, pl.ds(row, 1), :], (16, LANES)).astype(BF16)
            xm.append(x * jnp.concatenate([mask] * (C // 16), axis=0))
        p = dot(w_ref[slot, 0:4 * C, :], jnp.concatenate(xm, axis=1))
        for ab in range(2):
            for h in range(2):
                ls = slice(h * LANES, (h + 1) * LANES)
                val, gate = p[2 * ab * C:(2 * ab + 1) * C, ls], p[(2 * ab + 1) * C:(2 * ab + 2) * C, ls]
                s_ref[h, pl.ds(ab * C * ST + r, C, stride=ST), :] = val * (jnp.tanh(gate) + 1.0)

    def ab_copy(g):
        slot = g % 2
        return pltpu.make_async_remote_copy(
            abs_ref.at[slot], ab_ref.at[:, :, :, pl.ds(pl.multiple_of(mine + g * G, G), G), :],
            ab_send.at[slot], ab_recv.at[g], device_id=partner, device_id_type=MESH)

    def spread_ab(g):
        @pl.when(g >= 2)
        def _():
            ab_copy(g - 2).wait_send()

        own, other = side * CO, (1 - side) * CO
        rows = pl.ds(pl.multiple_of(mine + g * G, G), G)

        @pl.loop(0, CO, step=8)
        def _(c0):
            for dc in range(8):
                for ab in range(2):
                    for h in range(2):
                        c = c0 + dc
                        ab_ref[ab, c, h, rows, :] = s_ref[h, pl.ds((ab * C + own + c) * ST, G), :].astype(BF16)
                        abs_ref[g % 2, ab, c, h] = s_ref[h, pl.ds((ab * C + other + c) * ST, G), :].astype(BF16)

        ab_copy(g).start()

    def drain_ab():
        for g in range(NG - 2, NG):
            ab_copy(g).wait_send()

    TB = 8

    def t_copy(cb):
        return pltpu.make_async_remote_copy(
            ts_ref.at[pl.ds(cb * TB, TB)], t_ref.at[pl.ds(side * CO + cb * TB, TB)],
            t_send.at[cb], t_recv.at[cb], device_id=partner, device_id_type=MESH)

    def triangle(outgoing):
        @pl.loop(0, CO // TB)
        def _(cb):
            for dc in range(TB):
                c = cb * TB + dc
                b = jnp.concatenate([ab_ref[1, c, 0], ab_ref[1, c, 1]], axis=1)
                if outgoing:
                    theirs = pl.multiple_of(NR - mine, NR)
                    a = jnp.concatenate([jnp.concatenate([ab_ref[0, c, h, pl.ds(r0, NR), :] for h in range(2)], axis=1)
                                         for r0 in (mine, theirs)], axis=0)
                    t = dot(a, b, ((1,), (1,)))
                else:
                    a = jnp.concatenate([ab_ref[0, c, side], ab_ref[0, c, 1 - side]], axis=1)
                    t = dot(a, b, ((0,), (0,)))
                t = t.astype(BF16)
                for h in range(2):
                    ls = slice(h * LANES, (h + 1) * LANES)
                    t_ref[side * CO + c, h] = t[:NR, ls]
                    ts_ref[c, h] = t[NR:, ls]
            t_copy(cb).start()

    def recv_ab():
        for g in range(NG):
            ab_copy(g).wait_recv()

    def recv_t():
        for cb in range(CO // TB):
            t_copy(cb).wait_recv()

    def drain_t():
        for cb in range(CO // TB):
            t_copy(cb).wait_send()

    for cp in params(0):
        cp.wait()

    @pl.loop(0, NG)
    def _(g):
        @pl.loop(0, G, step=2)
        def _(r):
            for dr in range(2):
                row = g * G + r + dr
                start_row(g, r + dr, 0, [z_ref[row, 0], z_ref[row, 1]])
        spread_ab(g)
    drain_ab()

    @pl.loop(0, n_upd)
    def _(u):
        recv_ab()

        @pl.when(u % 2 == 0)
        def _():
            triangle(True)

        @pl.when(u % 2 == 1)
        def _():
            triangle(False)

        @pl.when(u < n_upd - 1)
        def _():
            for cp in params(u + 2):
                cp.start()

        slot = (u + 1) % 2
        for cp in params(u + 1):
            cp.wait()
        recv_t()

        @pl.when(u < n_upd - 1)
        def _():
            @pl.loop(0, NG)
            def _(g):
                swap_t(g)

                @pl.loop(0, G, step=2)
                def _(r):
                    for dr in range(2):
                        start_row(g, r + dr, slot, finish_row(g, r + dr, slot))
                spread_ab(g)
            drain_ab()
        drain_t()

    slot = n_upd % 2
    swap_t(q)

    @pl.loop(0, G, step=2)
    def _(r):
        for dr in range(2):
            finish_row(q, r + dr, slot)
    cp = pltpu.make_async_copy(z_ref.at[rows_of(q)], out, in_sem.at[0])
    cp.start()
    cp.wait()


def pack_params(norm_in, norm_out, w_ab, w_gate, w_out):
    n_upd = w_ab.shape[0] * 2

    def flat(w):
        return w.reshape((n_upd,) + w.shape[2:])

    wab, wg, wo = (jnp.swapaxes(flat(w) * jnp.asarray(0.5, BF16), 1, 2) for w in (w_ab, w_gate, w_out))
    w = jnp.zeros((n_upd + 1, 6 * C, C), BF16)
    w = w.at[:n_upd, :4 * C].set(wab).at[1:, 4 * C:5 * C].set(wg).at[1:, 5 * C:].set(wo)
    n = jnp.zeros((n_upd + 1, 4, C), F32)
    n = n.at[:n_upd, :2].set(flat(norm_in).astype(F32)).at[1:, 2:].set(flat(norm_out).astype(F32))
    return w, jnp.broadcast_to(n[..., None], n.shape + (LANES,))


def solution(mesh):
    nz, ny = mesh.shape["dap2"], mesh.shape["dap"] // 2
    row_spec = P(ALL_ROWS, None, None)
    mask_spec = P(ALL_ROWS, None)

    def local_stack(pair_rep, pair_mask, norm_in, norm_out, w_ab, w_gate, w_out):
        G, N = pair_rep.shape[:2]
        NR, n_upd = N // 2, 2 * w_ab.shape[0]
        chips = nz * ny
        w, n = pack_params(norm_in, norm_out, w_ab, w_gate, w_out)
        z = jnp.transpose(pair_rep.reshape(G, chips, 2, G, C), (0, 2, 4, 1, 3)).reshape(G, 2, C, NR)
        m = jnp.transpose(pair_mask.astype(F32).reshape(G, chips, 2, G), (2, 0, 1, 3)).reshape(2, G, NR)
        ST = G + 1
        anyspec = pl.BlockSpec(memory_space=pl.ANY)
        dma = pltpu.SemaphoreType.DMA
        n_gather = 2 * (nz - 1) + nz
        o = pl.pallas_call(
            functools.partial(kernel, nz, ny, n_upd),
            out_shape=jax.ShapeDtypeStruct(z.shape, BF16),
            in_specs=[anyspec] * 4,
            out_specs=anyspec,
            scratch_shapes=[
                pltpu.VMEM((NR, 2, C, LANES), BF16),
                pltpu.VMEM((NR, 2, C, LANES), BF16),
                pltpu.VMEM((2, CO, 2, N, LANES), BF16),
                pltpu.VMEM((C, 2, NR, LANES), BF16),
                pltpu.VMEM((CO, 2, NR, LANES), BF16),
                pltpu.VMEM((2, 2, CO, 2, G, LANES), BF16),
                pltpu.VMEM((2, 2 * C * ST, LANES), F32),
                pltpu.VMEM((2, G * Y_PITCH, LANES), F32),
                pltpu.VMEM((2, NR, LANES), F32),
                pltpu.VMEM((2, 6 * C, C), BF16),
                pltpu.VMEM((2, 4, C, LANES), F32),
                dma((2,)), dma((2, 2)),
                dma((n_gather,)), dma((n_gather,)), dma((n_gather,)), dma((n_gather,)),
                dma((2,)), dma((NR // G,)), dma((8,)), dma((8,)),
            ],
            compiler_params=pltpu.CompilerParams(collective_id=0, has_side_effects=True, vmem_limit_bytes=67043328),
        )(z, m, w, n)
        o = o.reshape(G, 2, C, chips, G)
        return jnp.transpose(o, (0, 3, 1, 4, 2)).reshape(G, N, C)

    return jax.shard_map(local_stack, mesh=mesh, in_specs=(row_spec, mask_spec, P(), P(), P(), P(), P()), out_specs=row_spec, check_vma=False)
```

time: 4360 us -> 1970 us (0.45)
  Pallas kernels: 0 us -> 1930 us
  blocking collectives: 1750 us -> 0 us
  local copies, waits for them, and re-layouts: 1280 us -> 27.1 us
  waiting for transfers between devices: 620 us -> 0 us
  matrix products: 342 us -> 0 us
  other arithmetic: 182 us -> 9.35 us
  starting transfers between devices: 142 us -> 0 us
    pallas_call x0 -> x1, Pallas kernels: none -> 1930 us  [local_stack(): pl.pallas_call(functools.partial(kernel, nz, ny, n_upd), out_shape=jax.Sh...]
    all_to_all x32 -> x0, blocking collectives: 1750 us -> none  [tri_update(): ab_cols = lax.all_to_all(ab_rows, ROW_AXES, 1, 2, tiled=True)]
    all_to_all x32 -> x0, waiting for transfers between devices: 620 us -> none  [tri_update(): tri_rows = lax.all_to_all(tri_full, ROW_AXES, 1, 0, tiled=True)]
    unnamed x249 -> x0, local copies, waits for them, and re-layouts: 506 us -> none
    slice x128 -> x0, local copies, waits for them, and re-layouts: 376 us -> none  [the longest x32 366 us: row_inputs(): proj_four[:, 1]]
    dot_general x128 -> x0, matrix products: 342 us -> none  [the longest x32 177 us: row_inputs(): jnp.einsum('de,ikd->eik', w_ab, x_ln, preferred_element_type=jnp.float32)]
    reshape x32 -> x4, local copies, waits for them, and re-layouts: 337 us -> 2.23 us  [the longest x1 1.31 us: local_stack(): jnp.transpose(pair_rep.reshape(G, chips, 2, G, C), (0, 2, 4, 1, 3))]
    convert_element_type x42 -> x1, other arithmetic: 156 us -> 0.72 us  [local_stack(): pair_mask.astype(F32).reshape(G, chips, 2, G)]
  transfers between devices with their start and end apart: 32 -> 0, of which waited for: 32 -> 0; matrix products, arithmetic and copies ran while one was open for 2% -> 0% of each run, Pallas kernels for 0% -> 0%
where the time goes in v1:
time: 1970 us
  Pallas kernels  1930 us (98%)
  local copies, waits for them, and re-layouts  27.1 us (1%)
    pallas_call x1, Pallas kernels, local_stack(): pl.pallas_call(functools.partial(kernel, nz, ny, n_upd), out_shape=jax.Sh...  1930 us

profile of v1, /device:TPU:0, one launch (start us, length us, event | category | flops | bytes accessed | tf_op | source)
XLA Modules:
  0.0 1969.5 jit_solution(13520350866965833630)
XLA Ops:
  0.0 0.7 convert_element_type.13
  0.7 0.7 pad_convert_fusion
  1.5 0.7 convert_dynamic-update-slice_fusion
  2.2 0.2 reshape.213
  2.4 0.7 reshape.214.m_in
  3.1 1.5 copy.20
  4.6 1.3 copy.25.z_in
  5.9 1.3 broadcast_multiply_fusion.2
  7.3 0.7 copy.23
  7.9 1.3 broadcast_multiply_fusion.1
  9.2 0.7 copy.24
  9.9 4.5 broadcast_multiply_fusion
  14.4 6.4 copy.22
  20.8 5.9 scatter.20
  26.8 1.2 constant_dynamic-update-slice_fusion.1
  27.9 1.2 constant_dynamic-update-slice_fusion.w_in
  29.1 4.6 broadcast_in_dim.2.n_in
  33.7 1933.0 %shard_map.73 = bf16[16,2,128,128]{3,2,1,0:T(8,128)(2,1)} custom-call(bf16[16,2,128,128]{3,2,1,0:T(8,128)(2,1)} %copy.25.z_in, f32[2,16,128]{2,1,0:T(8,128)} %reshape.214.m_in, bf16[33,768,128]{2,1,0:T(8,128)(2,1)} %constant_dynamic-update-slice_fusion.w_in, f32[33,4,128,128]{3,2,1,0:T(8,128)} %broadcast_in_dim.2.n_in), custom_call_target="tpu_custom_call" | custom-call | tf_op jit(solution)/shard_map/pallas_call | solution.py:345
  1966.7 1.6 copy.26
  1968.3 1.2 copy.27
  (1 shorter events, 0.0 us)

commit v2 on v0

v2 whole, which is shorter than its diff:
```python
import functools

import jax
import jax.numpy as jnp
from jax import lax
from jax.experimental import pallas as pl
from jax.experimental.pallas import tpu as pltpu
from jax.sharding import PartitionSpec as P

LN_EPS = 1e-5
ALL_ROWS = ("data", "dap2", "dap")
MESH = pl.DeviceIdType.MESH
F32, BF16 = jnp.float32, jnp.bfloat16
C = 128
CO = C // 2
LANES = 128
Y_PITCH = 132
R = 4
TB = 8


def total(v):
    parts = [v[32 * k:32 * k + 32] for k in range(4)]
    s = (parts[0] + parts[1]) + (parts[2] + parts[3])
    return jnp.sum(s, axis=0, keepdims=True)


def layer_norm(v, gain, shift):
    centered = v - total(v) * (1.0 / C)
    var = total(centered * centered) * (1.0 / C)
    return (centered * lax.rsqrt(var + LN_EPS) * gain + shift).astype(BF16)


def dot(lhs, rhs, dims=((1,), (0,))):
    return lax.dot_general(lhs, rhs, (dims, ((), ())), preferred_element_type=F32)


def half(h):
    return slice(h * LANES, (h + 1) * LANES)


def kernel(nz, ny, n_upd, z_in, m_in, norms, wab_in, wg_in, wo_in, out, z_ref, x_ref, ab_ref, t_ref, ts_ref, abs_ref,
           s_ref, y_ref, yb_ref, m_ref, mi_ref, wr_ref, w_ref, n_ref, in_sem, w_sem, zsend, zrecv, msend, mrecv,
           ab_send, ab_recv, t_send, t_recv):
    G = z_in.shape[0]
    NR = 2 * G * nz * ny // 2
    NG = NR // G
    ST = G + 1
    NB = NR // R
    BG = G // R
    chips = nz * ny
    zi = lax.axis_index("dap2")
    dap = lax.axis_index("dap")
    yi, side = dap // 2, dap % 2
    q = zi * ny + yi
    partner = {"dap": yi * 2 + 1 - side}
    ypeer = {"dap": (1 - yi) * 2 + side}
    up, down = {"dap2": zi + 1}, {"dap2": zi - 1}
    mine = pl.multiple_of(side * NR, NR)
    theirs = pl.multiple_of(NR - side * NR, NR)

    barrier = pltpu.get_barrier_semaphore()
    pl.semaphore_signal(barrier, inc=1, device_id=partner, device_id_type=MESH)
    if ny > 1:
        pl.semaphore_signal(barrier, inc=1, device_id=ypeer, device_id_type=MESH)

    @pl.when(zi < nz - 1)
    def _():
        pl.semaphore_signal(barrier, inc=1, device_id=up, device_id_type=MESH)

    @pl.when(zi > 0)
    def _():
        pl.semaphore_signal(barrier, inc=1, device_id=down, device_id_type=MESH)

    def rows_of(block):
        return pl.ds(pl.multiple_of(block * G, G), G)

    def weight_copies(s):
        now, before = jnp.minimum(s, n_upd - 1), jnp.clip(s - 1, 0, n_upd - 1)
        return (
            pltpu.make_async_copy(wab_in.at[now], wr_ref.at[:, pl.ds(0, 4 * C)], w_sem.at[0]),
            pltpu.make_async_copy(wg_in.at[before], wr_ref.at[:, pl.ds(4 * C, C)], w_sem.at[1]),
            pltpu.make_async_copy(wo_in.at[before], wr_ref.at[:, pl.ds(5 * C, C)], w_sem.at[2]),
        )

    def start(copies):
        for cp in copies:
            cp.start()

    def prepare(s):
        for cp in weight_copies(s):
            cp.wait()
        for k in range(6):
            w_ref[k * C:(k + 1) * C, :] = (wr_ref[:, k * C:(k + 1) * C] * jnp.asarray(0.5, BF16)).T
        now, before = jnp.minimum(s, n_upd - 1), jnp.clip(s - 1, 0, n_upd - 1)
        for k in range(2):
            n_ref[k] = jnp.broadcast_to(norms[pl.ds(now * 2 + k, 1), :], (C, C)).T
            n_ref[2 + k] = jnp.broadcast_to(norms[pl.ds((n_upd + before) * 2 + k, 1), :], (C, C)).T

    start(weight_copies(0))

    loads = (
        pltpu.make_async_copy(z_in, ts_ref.at[pl.ds(0, G)], in_sem.at[0]),
        pltpu.make_async_copy(m_in, mi_ref, in_sem.at[1]),
    )
    start(loads)
    for cp in loads:
        cp.wait()
    at = lax.broadcasted_iota(jnp.int32, (2 * NR, 2 * NR), 0)
    to = lax.broadcasted_iota(jnp.int32, (2 * NR, 2 * NR), 1)
    source = (to % NR) // G * (2 * G) + to // NR * G + to % G
    order = jnp.where(at == source, 1.0, 0.0).astype(BF16)
    m_perm = dot(mi_ref[...].astype(F32).astype(BF16), order)
    for h in range(2):
        m_ref[h, rows_of(q), :] = m_perm[:, half(h)]

    def pieces(h):
        return [divmod((k * 2 + h) * G, LANES) for k in range(chips)]

    @pl.loop(0, G)
    def _(r):
        for h in range(2):
            rows = [ts_ref[r, a, b:b + G, :] for a, b in pieces(h)]
            z_ref[q * G + r, h] = jnp.concatenate(rows, axis=0).T

    neighbours = (2 if ny > 1 else 1) + jnp.where(zi < nz - 1, 1, 0) + jnp.where(zi > 0, 1, 0)
    pl.semaphore_wait(barrier, neighbours)

    def block_copies(block, to, k):
        rows = rows_of(block)
        return (
            pltpu.make_async_remote_copy(z_ref.at[rows], z_ref.at[rows], zsend.at[k], zrecv.at[k], device_id=to, device_id_type=MESH),
            pltpu.make_async_remote_copy(m_ref.at[:, rows], m_ref.at[:, rows], msend.at[k], mrecv.at[k], device_id=to, device_id_type=MESH),
        )

    K_DOWN, K_Y = nz - 1, 2 * (nz - 1)

    def gather(d):
        if d == 0 and ny > 1:
            start(block_copies(q, ypeer, K_Y + zi))
        have_low, have_high = zi - d >= 0, zi + d <= nz - 1
        low, high = (zi - d) * ny + yi, (zi + d) * ny + yi
        if d > 0:
            @pl.when(have_low)
            def _():
                for cp in block_copies(low, up, d - 1):
                    cp.wait_recv()
                if ny > 1:
                    start(block_copies(low, ypeer, K_Y + zi - d))

            @pl.when(have_high)
            def _():
                for cp in block_copies(high, down, K_DOWN + d - 1):
                    cp.wait_recv()
                if ny > 1:
                    start(block_copies(high, ypeer, K_Y + zi + d))
        if d < nz - 1:
            @pl.when(jnp.logical_and(have_low, zi < nz - 1))
            def _():
                start(block_copies(low, up, d))

            @pl.when(jnp.logical_and(have_high, zi > 0))
            def _():
                start(block_copies(high, down, K_DOWN + d))

    for d in range(nz):
        gather(d)
    prepare(0)
    start(weight_copies(1))
    if ny > 1:
        for zz in range(nz):
            for cp in block_copies(zz * ny + 1 - yi, ypeer, K_Y + zz):
                cp.wait_recv()
    for d in range(nz - 1):
        @pl.when(jnp.logical_and(zi - d >= 0, zi < nz - 1))
        def _():
            for cp in block_copies((zi - d) * ny + yi, up, d):
                cp.wait_send()

        @pl.when(jnp.logical_and(zi + d <= nz - 1, zi > 0))
        def _():
            for cp in block_copies((zi + d) * ny + yi, down, K_DOWN + d):
                cp.wait_send()
    if ny > 1:
        for zz in range(nz):
            for cp in block_copies(zz * ny + yi, ypeer, K_Y + zz):
                cp.wait_send()

    def swap_t(g, c0, n, slot):
        t, y = t_ref.at[pl.ds(c0, n), :, rows_of(g), :], y_ref.at[slot]
        for dc in range(n):
            for h in range(2):
                y[h, pl.ds(c0 + dc, G, stride=Y_PITCH), :] = t[dc, h].astype(F32)

    def out_norm(r, slot):
        return [layer_norm(y_ref[slot, h, pl.ds(r * Y_PITCH, C), :], n_ref[2], n_ref[3]) for h in range(2)]

    def out_dots(row, y):
        upd = dot(w_ref[5 * C:6 * C, :], jnp.concatenate(y, axis=1))
        gate = dot(w_ref[4 * C:5 * C, :], jnp.concatenate([x_ref[row, 0], x_ref[row, 1]], axis=1))
        return upd, gate

    def new_z(row, upd, gate):
        z_row = [(z_ref[row, h].astype(F32) + (jnp.tanh(gate[:, half(h)]) + 1.0) * upd[:, half(h)]).astype(BF16) for h in range(2)]
        for h in range(2):
            z_ref[row, h] = z_row[h]
        return z_row

    def in_norm(row, z_row):
        for h in range(2):
            x_ref[row, h] = layer_norm(z_row[h].astype(F32), n_ref[0], n_ref[1])

    def ab_dot(row):
        x = []
        for h in range(2):
            mask = jnp.broadcast_to(m_ref[h, pl.ds(row, 1), :], (16, LANES)).astype(BF16)
            x.append(x_ref[row, h] * jnp.concatenate([mask] * (C // 16), axis=0))
        return dot(w_ref[0:4 * C, :], jnp.concatenate(x, axis=1))

    def ab_store(p, r, slot):
        for ab in range(2):
            for h in range(2):
                val, gate = p[2 * ab * C:(2 * ab + 1) * C, half(h)], p[(2 * ab + 1) * C:(2 * ab + 2) * C, half(h)]
                s_ref[slot, h, pl.ds(ab * C * ST + r, C, stride=ST), :] = val * (jnp.tanh(gate) + 1.0)

    CB = CO // BG
    LBG = BG.bit_length() - 1

    def ab_copy(k):
        c0 = pl.multiple_of((k & (BG - 1)) * CB, CB)
        rows = pl.ds(pl.multiple_of(mine + (k >> LBG) * G, G), G)
        return pltpu.make_async_remote_copy(
            abs_ref.at[(k & (BG - 1))], ab_ref.at[:, pl.ds(c0, CB), :, rows, :],
            ab_send.at[(k & (BG - 1))], ab_recv.at[(k & (BG - 1))], device_id=partner, device_id_type=MESH)

    def spread_ab(k):
        g, c0 = (k >> LBG), (k & (BG - 1)) * CB
        own, other = (side * CO + c0) * ST, ((1 - side) * CO + c0) * ST
        s = s_ref.at[(g & 1)]
        here = ab_ref.at[:, pl.ds(c0, CB), :, pl.ds(pl.multiple_of(mine + g * G, G), G), :]
        there = abs_ref.at[(k & (BG - 1))]
        for dc in range(CB):
            for ab in range(2):
                for h in range(2):
                    here[ab, dc, h] = s[h, pl.ds(own + (ab * C + dc) * ST, G), :].astype(BF16)
                    there[ab, dc, h] = s[h, pl.ds(other + (ab * C + dc) * ST, G), :].astype(BF16)

    def send_ab(k):
        @pl.when(k >= 0)
        def _():
            ab_copy(k).start()

        @pl.when(k + 1 >= BG)
        def _():
            ab_copy(k + 1 - BG).wait_send()

    def finish_ab():
        @pl.loop(NB - BG, NB)
        def _(k):
            spread_ab(k)
            send_ab(k)
        for k in range(NB - BG + 1, NB):
            ab_copy(k).wait_send()

    def t_copy(cb):
        n = CO // TB
        return pltpu.make_async_remote_copy(
            ts_ref.at[pl.ds(cb * n, n)], t_ref.at[pl.ds(side * CO + cb * n, n)],
            t_send.at[cb], t_recv.at[cb], device_id=partner, device_id_type=MESH)

    def triangle(outgoing, c):
        b = jnp.concatenate([ab_ref[1, c, 0], ab_ref[1, c, 1]], axis=1)
        if outgoing:
            a = jnp.concatenate([jnp.concatenate([ab_ref[0, c, h, pl.ds(r0, NR), :] for h in range(2)], axis=1)
                                 for r0 in (mine, theirs)], axis=0)
            t = dot(a, b, ((1,), (1,)))
        else:
            a = jnp.concatenate([ab_ref[0, c, side], ab_ref[0, c, 1 - side]], axis=1)
            t = dot(a, b, ((0,), (0,)))
        t = t.astype(BF16)
        for h in range(2):
            t_ref[side * CO + c, h] = t[:NR, half(h)]
            ts_ref[c, h] = t[NR:, half(h)]

    def triangles(outgoing):
        @pl.loop(0, TB)
        def _(cb):
            @pl.when(cb % (TB // BG) == 0 if BG < TB else cb >= 0)
            def _():
                for k in range(max(1, BG // TB)):
                    b = cb * BG // TB + k
                    arrived = ab_ref.at[:, pl.ds(b * CB, CB), :, pl.ds(theirs, NR), :]
                    pltpu.make_async_copy(arrived, arrived, ab_recv.at[b]).wait()
            for dc in range(CO // TB):
                triangle(outgoing, cb * (CO // TB) + dc)
            t_copy(cb).start()

    def step_row(it, behind):
        return jnp.where(it < behind, NR, (it - behind) * R)

    @pl.loop(0, NB + 1)
    def _(it):
        row, k = step_row(it, 1), it - 1 - BG
        dots = [ab_dot(row + i) for i in range(R)]
        spread_ab(jnp.maximum(k, 0))
        for i in range(R):
            in_norm(it * R + i, [z_ref[it * R + i, 0], z_ref[it * R + i, 1]])
        prev = it - 1 + 2 * BG
        for i in range(R):
            ab_store(dots[i], (prev & (BG - 1)) * R + i, ((prev >> LBG) & 1))
        send_ab(k)
    finish_ab()

    @pl.loop(0, n_upd)
    def _(u):
        @pl.when(u % 2 == 0)
        def _():
            triangles(True)

        @pl.when(u % 2 == 1)
        def _():
            triangles(False)

        prepare(u + 1)
        start(weight_copies(u + 2))
        for cb in range(TB):
            t_copy(cb).wait_recv()

        @pl.when(u < n_upd - 1)
        def _():
            for c0 in range(0, C, 16):
                swap_t(0, c0, 16, 0)

            @pl.loop(0, NB + 2)
            def _(it):
                k = it - 2 - BG
                row1, row2 = step_row(it, 1), step_row(it, 2)
                outs = [out_dots(row1 + i, [yb_ref[(it + 1) & 1, i, h] for h in range(2)]) for i in range(R)]
                dots = [ab_dot(row2 + i) for i in range(R)]
                for i in range(R):
                    y = out_norm((it & (BG - 1)) * R + i, (it >> LBG) & 1)
                    for h in range(2):
                        yb_ref[it & 1, i, h] = y[h]
                spread_ab(jnp.maximum(k, 0))
                swap_t(jnp.minimum((it >> LBG) + 1, NG - 1), (it & (BG - 1)) * (C // BG), C // BG, ((it >> LBG) + 1) & 1)
                for i in range(R):
                    in_norm(row1 + i, new_z(row1 + i, *outs[i]))
                prev = it - 2 + 2 * BG
                for i in range(R):
                    ab_store(dots[i], (prev & (BG - 1)) * R + i, (prev >> LBG) & 1)
                send_ab(k)
            finish_ab()
        for cb in range(TB):
            t_copy(cb).wait_send()

    for cp in weight_copies(0):
        cp.wait()
    for c0 in range(0, C, 16):
        swap_t(q, c0, 16, 0)

    @pl.loop(0, G)
    def _(r):
        row = q * G + r
        z_row = new_z(row, *out_dots(row, out_norm(r, 0)))
        for h in range(2):
            z_t = z_row[h].T
            for k, (a, b) in enumerate(pieces(h)):
                ts_ref[r, a, b:b + G, :] = z_t[k * G:(k + 1) * G]
    cp = pltpu.make_async_copy(ts_ref.at[pl.ds(0, G)], out, in_sem.at[0])
    cp.start()
    cp.wait()


def solution(mesh):
    nz, ny = mesh.shape["dap2"], mesh.shape["dap"] // 2
    row_spec = P(ALL_ROWS, None, None)
    mask_spec = P(ALL_ROWS, None)

    def local_stack(pair_rep, pair_mask, norm_in, norm_out, w_ab, w_gate, w_out):
        G, N = pair_rep.shape[:2]
        NR, n_upd = N // 2, 2 * w_ab.shape[0]
        norms = jnp.concatenate([norm_in.reshape(-1, C), norm_out.reshape(-1, C)]).astype(F32)
        BG = G // R
        anyspec = pl.BlockSpec(memory_space=pl.ANY)
        vmem = pl.BlockSpec(memory_space=pltpu.VMEM)
        dma = pltpu.SemaphoreType.DMA
        n_gather = 2 * (nz - 1) + nz
        o = pl.pallas_call(
            functools.partial(kernel, nz, ny, n_upd),
            out_shape=jax.ShapeDtypeStruct((G, 2, NR, C), BF16),
            in_specs=[anyspec, anyspec, vmem, anyspec, anyspec, anyspec],
            out_specs=anyspec,
            scratch_shapes=[
                pltpu.VMEM((NR + R, 2, C, LANES), BF16),
                pltpu.VMEM((NR + R, 2, C, LANES), BF16),
                pltpu.VMEM((2, CO, 2, N, LANES), BF16),
                pltpu.VMEM((C, 2, NR, LANES), BF16),
                pltpu.VMEM((CO, 2, NR, LANES), BF16),
                pltpu.VMEM((BG, 2, CO // BG, 2, G, LANES), BF16),
                pltpu.VMEM((2, 2, 2 * C * (G + 1), LANES), F32),
                pltpu.VMEM((2, 2, G * Y_PITCH, LANES), F32),
                pltpu.VMEM((2, R, 2, C, LANES), BF16),
                pltpu.VMEM((2, NR + R, LANES), F32),
                pltpu.VMEM((G, N), jnp.int32),
                pltpu.VMEM((C, 6 * C), BF16),
                pltpu.VMEM((6 * C, C), BF16),
                pltpu.VMEM((4, C, LANES), F32),
                dma((2,)), dma((3,)),
                dma((n_gather,)), dma((n_gather,)), dma((n_gather,)), dma((n_gather,)),
                dma((BG,)), dma((BG,)), dma((TB,)), dma((TB,)),
            ],
            compiler_params=pltpu.CompilerParams(collective_id=0, has_side_effects=True, vmem_limit_bytes=67043328),
        )(pair_rep.reshape(G, 2, NR, C), pair_mask, norms, w_ab.reshape(n_upd, C, 4 * C), w_gate.reshape(n_upd, C, C), w_out.reshape(n_upd, C, C))
        return o.reshape(G, N, C)

    return jax.shard_map(local_stack, mesh=mesh, in_specs=(row_spec, mask_spec, P(), P(), P(), P(), P()), out_specs=row_spec, check_vma=False)
```

time: 4360 us -> 1460 us (0.33)
  blocking collectives: 1750 us -> 0 us
  Pallas kernels: 0 us -> 1460 us
  local copies, waits for them, and re-layouts: 1280 us -> 2.3 us
  waiting for transfers between devices: 620 us -> 0 us
  matrix products: 342 us -> 0 us
  other arithmetic: 182 us -> 1.37 us
  starting transfers between devices: 142 us -> 0 us
    all_to_all x32 -> x0, blocking collectives: 1750 us -> none  [tri_update(): ab_cols = lax.all_to_all(ab_rows, ROW_AXES, 1, 2, tiled=True)]
    pallas_call x0 -> x1, Pallas kernels: none -> 1460 us  [local_stack(): pl.pallas_call(functools.partial(kernel, nz, ny, n_upd), out_shape=jax.Sh...]
    all_to_all x32 -> x0, waiting for transfers between devices: 620 us -> none  [tri_update(): tri_rows = lax.all_to_all(tri_full, ROW_AXES, 1, 0, tiled=True)]
    unnamed x249 -> x1, local copies, waits for them, and re-layouts: 506 us -> 2.3 us
    slice x128 -> x0, local copies, waits for them, and re-layouts: 376 us -> none  [the longest x32 366 us: row_inputs(): proj_four[:, 1]]
    dot_general x128 -> x0, matrix products: 342 us -> none  [the longest x32 177 us: row_inputs(): jnp.einsum('de,ikd->eik', w_ab, x_ln, preferred_element_type=jnp.float32)]
    reshape x32 -> x0, local copies, waits for them, and re-layouts: 337 us -> none  [row_inputs(): proj_all.reshape(2, 2, hidden, pair_loc.shape[0], pair_loc.shape[1])]
    convert_element_type x42 -> x1, other arithmetic: 156 us -> 1.37 us  [local_stack(): jnp.concatenate([norm_in.reshape(-1, C), norm_out.reshape(-1, C)])]
  transfers between devices with their start and end apart: 32 -> 0, of which waited for: 32 -> 0; matrix products, arithmetic and copies ran while one was open for 2% -> 0% of each run, Pallas kernels for 0% -> 0%
where the time goes in v2:
time: 1460 us
  Pallas kernels  1460 us (100%)
    pallas_call x1, Pallas kernels, local_stack(): pl.pallas_call(functools.partial(kernel, nz, ny, n_upd), out_shape=jax.Sh...  1460 us

profile of v2, /device:TPU:0, one launch (start us, length us, event | category | flops | bytes accessed | tf_op | source)
XLA Modules:
  0.0 1463.0 jit_solution(16610116331250453668)
XLA Ops:
  0.0 1.4 maximum_convert_fusion.norms
  1.4 1459.4 %shard_map.73 = bf16[16,2,128,128]{3,2,1,0:T(8,128)(2,1)} custom-call(bf16[16,2,128,128]{3,2,1,0:T(8,128)(2,1)} %bitcast.9, s32[16,256]{1,0:T(8,128)} %m_in.1, f32[128,128]{1,0:T(8,128)} %maximum_convert_fusion.norms, bf16[32,128,512]{2,1,0:T(8,128)(2,1)} %bitcast.7, bf16[32,128,128]{2,1,0:T(8,128)(2,1)} %bitcast.10, bf16[32,128,128]{2,1,0:T(8,128)(2,1)} %bitcast.11), custom_call_target="tpu_custom_call" | custom-call | tf_op jit(solution)/shard_map/pallas_call | solution.py:388
  1460.7 2.3 copy.9

commit v3 on v2

--- a/solution.py
+++ b/solution.py
@@ -117,11 +117,12 @@
     def pieces(h):
         return [divmod((k * 2 + h) * G, LANES) for k in range(chips)]
 
-    @pl.loop(0, G)
-    def _(r):
-        for h in range(2):
-            rows = [ts_ref[r, a, b:b + G, :] for a, b in pieces(h)]
-            z_ref[q * G + r, h] = jnp.concatenate(rows, axis=0).T
+    @pl.loop(0, G, step=4)
+    def _(r0):
+        for i in range(4):
+            for h in range(2):
+                rows = [ts_ref[r0 + i, a, b:b + G, :] for a, b in pieces(h)]
+                z_ref[q * G + r0 + i, h] = jnp.concatenate(rows, axis=0).T
 
     neighbours = (2 if ny > 1 else 1) + jnp.where(zi < nz - 1, 1, 0) + jnp.where(zi > 0, 1, 0)
     pl.semaphore_wait(barrier, neighbours)
@@ -163,28 +164,51 @@
             def _():
                 start(block_copies(high, down, K_DOWN + d))
 
-    for d in range(nz):
-        gather(d)
+    def nearest(k):
+        order = [sorted(range(nz), key=lambda z: (abs(z - me), z)) for me in range(nz)]
+        return sum(jnp.where(zi == me, order[me][k], 0) for me in range(nz))
+
+    arrivals = [(q, [lambda: gather(0)])]
+    for k in range(1, nz):
+        arrivals.append((nearest(k) * ny + yi, [functools.partial(gather, k)]))
+        if ny > 1:
+            arrivals.append((nearest(k - 1) * ny + 1 - yi, []))
+    if ny > 1:
+        arrivals.append((nearest(nz - 1) * ny + 1 - yi, []))
+
+    def await_y(block):
+        for cp in block_copies(block, ypeer, K_Y + block // ny):
+            cp.wait_recv()
+
+    def arrived(pos):
+        block, calls = arrivals[pos]
+        for call in calls:
+            call()
+        if not calls:
+            await_y(block)
+
+    def first_group(pos):
+        return sum(jnp.where(pos == k, block, 0) for k, (block, _) in enumerate(arrivals))
+
+    def drain_gather():
+        for d in range(nz - 1):
+            @pl.when(jnp.logical_and(zi - d >= 0, zi < nz - 1))
+            def _():
+                for cp in block_copies((zi - d) * ny + yi, up, d):
+                    cp.wait_send()
+
+            @pl.when(jnp.logical_and(zi + d <= nz - 1, zi > 0))
+            def _():
+                for cp in block_copies((zi + d) * ny + yi, down, K_DOWN + d):
+                    cp.wait_send()
+        if ny > 1:
+            for zz in range(nz):
+                for cp in block_copies(zz * ny + yi, ypeer, K_Y + zz):
+                    cp.wait_send()
+
+    arrived(0)
     prepare(0)
     start(weight_copies(1))
-    if ny > 1:
-        for zz in range(nz):
-            for cp in block_copies(zz * ny + 1 - yi, ypeer, K_Y + zz):
-                cp.wait_recv()
-    for d in range(nz - 1):
-        @pl.when(jnp.logical_and(zi - d >= 0, zi < nz - 1))
-        def _():
-            for cp in block_copies((zi - d) * ny + yi, up, d):
-                cp.wait_send()
-
-        @pl.when(jnp.logical_and(zi + d <= nz - 1, zi > 0))
-        def _():
-            for cp in block_copies((zi + d) * ny + yi, down, K_DOWN + d):
-                cp.wait_send()
-    if ny > 1:
-        for zz in range(nz):
-            for cp in block_copies(zz * ny + yi, ypeer, K_Y + zz):
-                cp.wait_send()
 
     def swap_t(g, c0, n, slot):
         t, y = t_ref.at[pl.ds(c0, n), :, rows_of(g), :], y_ref.at[slot]
@@ -226,18 +250,21 @@
     CB = CO // BG
     LBG = BG.bit_length() - 1
 
-    def ab_copy(k):
+    def same(g):
+        return g
+
+    def ab_copy(k, group=same):
         c0 = pl.multiple_of((k & (BG - 1)) * CB, CB)
-        rows = pl.ds(pl.multiple_of(mine + (k >> LBG) * G, G), G)
+        rows = pl.ds(pl.multiple_of(mine + group(k >> LBG) * G, G), G)
         return pltpu.make_async_remote_copy(
             abs_ref.at[(k & (BG - 1))], ab_ref.at[:, pl.ds(c0, CB), :, rows, :],
             ab_send.at[(k & (BG - 1))], ab_recv.at[(k & (BG - 1))], device_id=partner, device_id_type=MESH)
 
-    def spread_ab(k):
+    def spread_ab(k, group=same):
         g, c0 = (k >> LBG), (k & (BG - 1)) * CB
         own, other = (side * CO + c0) * ST, ((1 - side) * CO + c0) * ST
         s = s_ref.at[(g & 1)]
-        here = ab_ref.at[:, pl.ds(c0, CB), :, pl.ds(pl.multiple_of(mine + g * G, G), G), :]
+        here = ab_ref.at[:, pl.ds(c0, CB), :, pl.ds(pl.multiple_of(mine + group(g) * G, G), G), :]
         there = abs_ref.at[(k & (BG - 1))]
         for dc in range(CB):
             for ab in range(2):
@@ -245,28 +272,41 @@
                     here[ab, dc, h] = s[h, pl.ds(own + (ab * C + dc) * ST, G), :].astype(BF16)
                     there[ab, dc, h] = s[h, pl.ds(other + (ab * C + dc) * ST, G), :].astype(BF16)
 
-    def send_ab(k):
+    def send_ab(k, group=same):
         @pl.when(k >= 0)
         def _():
-            ab_copy(k).start()
+            ab_copy(k, group).start()
 
         @pl.when(k + 1 >= BG)
         def _():
-            ab_copy(k + 1 - BG).wait_send()
-
-    def finish_ab():
+            ab_copy(k + 1 - BG, group).wait_send()
+
+    def finish_ab(group=same):
         @pl.loop(NB - BG, NB)
         def _(k):
-            spread_ab(k)
-            send_ab(k)
+            spread_ab(k, group)
+            send_ab(k, group)
+
+    def drain_ab():
         for k in range(NB - BG + 1, NB):
             ab_copy(k).wait_send()
 
-    def t_copy(cb):
-        n = CO // TB
+    EARLY = min(2, NG) * G
+
+    def t_copy(c0, n, row0, rows, k):
+        c0, rows = pl.multiple_of(c0, n), pl.ds(row0, rows)
         return pltpu.make_async_remote_copy(
-            ts_ref.at[pl.ds(cb * n, n)], t_ref.at[pl.ds(side * CO + cb * n, n)],
-            t_send.at[cb], t_recv.at[cb], device_id=partner, device_id_type=MESH)
+            ts_ref.at[pl.ds(c0, n), :, rows, :], t_ref.at[pl.ds(side * CO + c0, n), :, rows, :],
+            t_send.at[k], t_recv.at[k], device_id=partner, device_id_type=MESH)
+
+    def early_t():
+        return t_copy(0, CO, 0, EARLY, 0)
+
+    def late_t(g):
+        return t_copy(0, CO, pl.multiple_of(g * G, G), G, g)
+
+    def recv_t(g):
+        late_t(g).wait_recv()
 
     def triangle(outgoing, c):
         b = jnp.concatenate([ab_ref[1, c, 0], ab_ref[1, c, 1]], axis=1)
@@ -293,38 +333,51 @@
                     pltpu.make_async_copy(arrived, arrived, ab_recv.at[b]).wait()
             for dc in range(CO // TB):
                 triangle(outgoing, cb * (CO // TB) + dc)
-            t_copy(cb).start()
+            t_copy(cb * (CO // TB), CO // TB, 0, EARLY, 0).start()
+        for g in range(EARLY // G, NG):
+            late_t(g).start()
 
     def step_row(it, behind):
         return jnp.where(it < behind, NR, (it - behind) * R)
 
     @pl.loop(0, NB + 1)
     def _(it):
-        row, k = step_row(it, 1), it - 1 - BG
+        for pos in range(1, len(arrivals)):
+            @pl.when(it == pos * BG)
+            def _(pos=pos):
+                arrived(pos)
+
+        def row_of(step):
+            return first_group(step >> LBG) * G + (step & (BG - 1)) * R
+
+        k = it - 1 - BG
+        row, now = jnp.where(it == 0, NR, row_of(it - 1)), jnp.where(it == NB, NR, row_of(it))
         dots = [ab_dot(row + i) for i in range(R)]
-        spread_ab(jnp.maximum(k, 0))
+        spread_ab(jnp.maximum(k, 0), first_group)
         for i in range(R):
-            in_norm(it * R + i, [z_ref[it * R + i, 0], z_ref[it * R + i, 1]])
+            in_norm(now + i, [z_ref[now + i, 0], z_ref[now + i, 1]])
         prev = it - 1 + 2 * BG
         for i in range(R):
-            ab_store(dots[i], (prev & (BG - 1)) * R + i, ((prev >> LBG) & 1))
-        send_ab(k)
-    finish_ab()
+            ab_store(dots[i], (prev & (BG - 1)) * R + i, (prev >> LBG) & 1)
+        send_ab(k, first_group)
+    finish_ab(first_group)
+    drain_gather()
 
     @pl.loop(0, n_upd)
     def _(u):
-        @pl.when(u % 2 == 0)
-        def _():
-            triangles(True)
-
-        @pl.when(u % 2 == 1)
-        def _():
-            triangles(False)
-
         prepare(u + 1)
         start(weight_copies(u + 2))
-        for cb in range(TB):
-            t_copy(cb).wait_recv()
+
+        @pl.when(u % 2 == 0)
+        def _():
+            triangles(True)
+
+        @pl.when(u % 2 == 1)
+        def _():
+            triangles(False)
+
+        drain_ab()
+        early_t().wait_recv()
 
         @pl.when(u < n_upd - 1)
         def _():
@@ -349,23 +402,34 @@
                 for i in range(R):
                     ab_store(dots[i], (prev & (BG - 1)) * R + i, (prev >> LBG) & 1)
                 send_ab(k)
+
+                @pl.when(jnp.logical_and(((it + 1) & (BG - 1)) == 0, it + 1 < NB - BG))
+                def _():
+                    recv_t(((it + 1) >> LBG) + 1)
             finish_ab()
-        for cb in range(TB):
-            t_copy(cb).wait_send()
+
+        @pl.when(u == n_upd - 1)
+        def _():
+            for g in range(EARLY // G, NG):
+                recv_t(g)
+        early_t().wait_send()
+        for g in range(EARLY // G, NG):
+            late_t(g).wait_send()
 
     for cp in weight_copies(0):
         cp.wait()
     for c0 in range(0, C, 16):
         swap_t(q, c0, 16, 0)
 
-    @pl.loop(0, G)
-    def _(r):
-        row = q * G + r
-        z_row = new_z(row, *out_dots(row, out_norm(r, 0)))
-        for h in range(2):
-            z_t = z_row[h].T
-            for k, (a, b) in enumerate(pieces(h)):
-                ts_ref[r, a, b:b + G, :] = z_t[k * G:(k + 1) * G]
+    @pl.loop(0, G, step=4)
+    def _(r0):
+        outs = [out_dots(q * G + r0 + i, out_norm(r0 + i, 0)) for i in range(4)]
+        for i in range(4):
+            z_row = new_z(q * G + r0 + i, *outs[i])
+            for h in range(2):
+                z_t = z_row[h].T
+                for k, (a, b) in enumerate(pieces(h)):
+                    ts_ref[r0 + i, a, b:b + G, :] = z_t[k * G:(k + 1) * G]
     cp = pltpu.make_async_copy(ts_ref.at[pl.ds(0, G)], out, in_sem.at[0])
     cp.start()
     cp.wait()
@@ -407,7 +471,7 @@
                 pltpu.VMEM((4, C, LANES), F32),
                 dma((2,)), dma((3,)),
                 dma((n_gather,)), dma((n_gather,)), dma((n_gather,)), dma((n_gather,)),
-                dma((BG,)), dma((BG,)), dma((TB,)), dma((TB,)),
+                dma((BG,)), dma((BG,)), dma((NR // G,)), dma((NR // G,)),
             ],
             compiler_params=pltpu.CompilerParams(collective_id=0, has_side_effects=True, vmem_limit_bytes=67043328),
         )(pair_rep.reshape(G, 2, NR, C), pair_mask, norms, w_ab.reshape(n_upd, C, 4 * C), w_gate.reshape(n_upd, C, C), w_out.reshape(n_upd, C, C))

time: 1460 us -> 1340 us (0.918)
  Pallas kernels: 1460 us -> 1340 us
    pallas_call x1, Pallas kernels: 1460 us -> 1340 us  [local_stack(): pl.pallas_call(functools.partial(kernel, nz, ny, n_upd), out_shape=jax.Sh...]
where the time goes in v3:
time: 1340 us
  Pallas kernels  1340 us (100%)
    pallas_call x1, Pallas kernels, local_stack(): pl.pallas_call(functools.partial(kernel, nz, ny, n_upd), out_shape=jax.Sh...  1340 us

profile of v3, /device:TPU:0, one launch (start us, length us, event | category | flops | bytes accessed | tf_op | source)
XLA Modules:
  0.0 1341.0 jit_solution(2763199794156604099)
XLA Ops:
  0.0 1.4 maximum_convert_fusion.norms
  1.4 1337.3 %shard_map.73 = bf16[16,2,128,128]{3,2,1,0:T(8,128)(2,1)} custom-call(bf16[16,2,128,128]{3,2,1,0:T(8,128)(2,1)} %bitcast.9, s32[16,256]{1,0:T(8,128)} %m_in.1, f32[128,128]{1,0:T(8,128)} %maximum_convert_fusion.norms, bf16[32,128,512]{2,1,0:T(8,128)(2,1)} %bitcast.7, bf16[32,128,128]{2,1,0:T(8,128)(2,1)} %bitcast.10, bf16[32,128,128]{2,1,0:T(8,128)(2,1)} %bitcast.11), custom_call_target="tpu_custom_call" | custom-call | tf_op jit(solution)/shard_map/pallas_call | solution.py:452
  1338.7 2.3 copy.9

commit v4 on v3

--- a/solution.py
+++ b/solution.py
@@ -14,9 +14,14 @@
 C = 128
 CO = C // 2
 LANES = 128
-Y_PITCH = 132
+Y_PITCH = 129
 R = 4
-TB = 8
+TB = 4
+ORDER = (
+    ("u", 0), ("g", 0), ("a", 0), ("g", 2), ("u", 2), ("a", 2),
+    ("u", 1), ("u", 3), ("g", 1), ("a", 1), ("g", 3), ("a", 3),
+)
+WB = 16
 
 
 def total(v):
@@ -91,7 +96,13 @@
         for cp in weight_copies(s):
             cp.wait()
         for k in range(6):
-            w_ref[k * C:(k + 1) * C, :] = (wr_ref[:, k * C:(k + 1) * C] * jnp.asarray(0.5, BF16)).T
+            w = (wr_ref[:, k * C:(k + 1) * C] * jnp.asarray(0.5, BF16)).T
+            if k >= 4:
+                w_ref[k * C:(k + 1) * C, :] = w
+            else:
+                for c in range(0, C, WB):
+                    at = k // 2 * 2 * C + 2 * c + k % 2 * WB
+                    w_ref[at:at + WB, :] = w[c:c + WB]
         now, before = jnp.minimum(s, n_upd - 1), jnp.clip(s - 1, 0, n_upd - 1)
         for k in range(2):
             n_ref[k] = jnp.broadcast_to(norms[pl.ds(now * 2 + k, 1), :], (C, C)).T
@@ -219,10 +230,11 @@
     def out_norm(r, slot):
         return [layer_norm(y_ref[slot, h, pl.ds(r * Y_PITCH, C), :], n_ref[2], n_ref[3]) for h in range(2)]
 
-    def out_dots(row, y):
-        upd = dot(w_ref[5 * C:6 * C, :], jnp.concatenate(y, axis=1))
-        gate = dot(w_ref[4 * C:5 * C, :], jnp.concatenate([x_ref[row, 0], x_ref[row, 1]], axis=1))
-        return upd, gate
+    def upd_dot(y):
+        return dot(w_ref[5 * C:6 * C, :], jnp.concatenate(y, axis=1))
+
+    def gate_dot(row):
+        return dot(w_ref[4 * C:5 * C, :], jnp.concatenate([x_ref[row, 0], x_ref[row, 1]], axis=1))
 
     def new_z(row, upd, gate):
         z_row = [(z_ref[row, h].astype(F32) + (jnp.tanh(gate[:, half(h)]) + 1.0) * upd[:, half(h)]).astype(BF16) for h in range(2)]
@@ -244,8 +256,10 @@
     def ab_store(p, r, slot):
         for ab in range(2):
             for h in range(2):
-                val, gate = p[2 * ab * C:(2 * ab + 1) * C, half(h)], p[(2 * ab + 1) * C:(2 * ab + 2) * C, half(h)]
-                s_ref[slot, h, pl.ds(ab * C * ST + r, C, stride=ST), :] = val * (jnp.tanh(gate) + 1.0)
+                for c in range(0, C, WB):
+                    at = 2 * (ab * C + c)
+                    val, gate = p[at:at + WB, half(h)], p[at + WB:at + 2 * WB, half(h)]
+                    s_ref[slot, h, pl.ds((ab * C + c) * ST + r, WB, stride=ST), :] = val * (jnp.tanh(gate) + 1.0)
 
     CB = CO // BG
     LBG = BG.bit_length() - 1
@@ -334,11 +348,8 @@
             for dc in range(CO // TB):
                 triangle(outgoing, cb * (CO // TB) + dc)
             t_copy(cb * (CO // TB), CO // TB, 0, EARLY, 0).start()
-        for g in range(EARLY // G, NG):
+        for g in range(EARLY // G, min(EARLY // G + 2, NG)):
             late_t(g).start()
-
-    def step_row(it, behind):
-        return jnp.where(it < behind, NR, (it - behind) * R)
 
     @pl.loop(0, NB + 1)
     def _(it):
@@ -351,7 +362,7 @@
             return first_group(step >> LBG) * G + (step & (BG - 1)) * R
 
         k = it - 1 - BG
-        row, now = jnp.where(it == 0, NR, row_of(it - 1)), jnp.where(it == NB, NR, row_of(it))
+        row, now = row_of(jnp.maximum(it - 1, 0)), row_of(jnp.minimum(it, NB - 1))
         dots = [ab_dot(row + i) for i in range(R)]
         spread_ab(jnp.maximum(k, 0), first_group)
         for i in range(R):
@@ -384,32 +395,59 @@
             for c0 in range(0, C, 16):
                 swap_t(0, c0, 16, 0)
 
-            @pl.loop(0, NB + 2)
-            def _(it):
-                k = it - 2 - BG
-                row1, row2 = step_row(it, 1), step_row(it, 2)
-                outs = [out_dots(row1 + i, [yb_ref[(it + 1) & 1, i, h] for h in range(2)]) for i in range(R)]
-                dots = [ab_dot(row2 + i) for i in range(R)]
+            def norm_rows(it):
                 for i in range(R):
                     y = out_norm((it & (BG - 1)) * R + i, (it >> LBG) & 1)
                     for h in range(2):
                         yb_ref[it & 1, i, h] = y[h]
-                spread_ab(jnp.maximum(k, 0))
                 swap_t(jnp.minimum((it >> LBG) + 1, NG - 1), (it & (BG - 1)) * (C // BG), C // BG, ((it >> LBG) + 1) & 1)
-                for i in range(R):
-                    in_norm(row1 + i, new_z(row1 + i, *outs[i]))
+
+            def store_rows(it, dots):
                 prev = it - 2 + 2 * BG
                 for i in range(R):
                     ab_store(dots[i], (prev & (BG - 1)) * R + i, (prev >> LBG) & 1)
+
+            norm_rows(0)
+
+            @pl.loop(1, NB + 1)
+            def _(it):
+                k = it - 2 - BG
+                row1, row2 = (it - 1) * R, jnp.maximum(it - 2, 0) * R
+                parts = {}
+                for part, i in ORDER:
+                    if part == "u":
+                        parts["u", i] = upd_dot([yb_ref[(it + 1) & 1, i, h] for h in range(2)])
+                    elif part == "g":
+                        parts["g", i] = gate_dot(row1 + i)
+                    else:
+                        parts["a", i] = ab_dot(row2 + i)
+                spread_ab(jnp.maximum(k, 0))
+                norm_rows(it)
+                for i in range(R):
+                    in_norm(row1 + i, new_z(row1 + i, parts["u", i], parts["g", i]))
+                store_rows(it, [parts["a", i] for i in range(R)])
                 send_ab(k)
 
-                @pl.when(jnp.logical_and(((it + 1) & (BG - 1)) == 0, it + 1 < NB - BG))
+                g = ((it + 1) >> LBG) + 1
+
+                @pl.when(jnp.logical_and(((it + 1) & (BG - 1)) == 0, g < NG - 2))
                 def _():
-                    recv_t(((it + 1) >> LBG) + 1)
+                    late_t(g + 2).start()
+
+                @pl.when(jnp.logical_and(((it + 1) & (BG - 1)) == 0, g < NG))
+                def _():
+                    recv_t(g)
+
+            dots = [ab_dot((NB - 1) * R + i) for i in range(R)]
+            spread_ab(NB - 1 - BG)
+            store_rows(NB + 1, dots)
+            send_ab(NB - 1 - BG)
             finish_ab()
 
         @pl.when(u == n_upd - 1)
         def _():
+            for g in range(EARLY // G + 2, NG):
+                late_t(g).start()
             for g in range(EARLY // G, NG):
                 recv_t(g)
         early_t().wait_send()
@@ -423,7 +461,7 @@
 
     @pl.loop(0, G, step=4)
     def _(r0):
-        outs = [out_dots(q * G + r0 + i, out_norm(r0 + i, 0)) for i in range(4)]
+        outs = [(upd_dot(out_norm(r0 + i, 0)), gate_dot(q * G + r0 + i)) for i in range(4)]
         for i in range(4):
             z_row = new_z(q * G + r0 + i, *outs[i])
             for h in range(2):
@@ -455,8 +493,8 @@
             in_specs=[anyspec, anyspec, vmem, anyspec, anyspec, anyspec],
             out_specs=anyspec,
             scratch_shapes=[
-                pltpu.VMEM((NR + R, 2, C, LANES), BF16),
-                pltpu.VMEM((NR + R, 2, C, LANES), BF16),
+                pltpu.VMEM((NR, 2, C, LANES), BF16),
+                pltpu.VMEM((NR, 2, C, LANES), BF16),
                 pltpu.VMEM((2, CO, 2, N, LANES), BF16),
                 pltpu.VMEM((C, 2, NR, LANES), BF16),
                 pltpu.VMEM((CO, 2, NR, LANES), BF16),
@@ -464,7 +502,7 @@
                 pltpu.VMEM((2, 2, 2 * C * (G + 1), LANES), F32),
                 pltpu.VMEM((2, 2, G * Y_PITCH, LANES), F32),
                 pltpu.VMEM((2, R, 2, C, LANES), BF16),
-                pltpu.VMEM((2, NR + R, LANES), F32),
+                pltpu.VMEM((2, NR, LANES), F32),
                 pltpu.VMEM((G, N), jnp.int32),
                 pltpu.VMEM((C, 6 * C), BF16),
                 pltpu.VMEM((6 * C, C), BF16),

time: 1340 us -> 1130 us (0.84)
  Pallas kernels: 1340 us -> 1130 us
    pallas_call x1, Pallas kernels: 1340 us -> 1130 us  [local_stack(): pl.pallas_call(functools.partial(kernel, nz, ny, n_upd), out_shape=jax.Sh...]
where the time goes in v4:
time: 1130 us
  Pallas kernels  1130 us (100%)
    pallas_call x1, Pallas kernels, local_stack(): pl.pallas_call(functools.partial(kernel, nz, ny, n_upd), out_shape=jax.Sh...  1130 us

profile of v4, /device:TPU:0, one launch (start us, length us, event | category | flops | bytes accessed | tf_op | source)
XLA Modules:
  0.0 1130.4 jit_solution(9117276605613381090)
XLA Ops:
  0.0 1.4 maximum_convert_fusion.norms
  1.4 1126.7 %shard_map.73 = bf16[16,2,128,128]{3,2,1,0:T(8,128)(2,1)} custom-call(bf16[16,2,128,128]{3,2,1,0:T(8,128)(2,1)} %bitcast.9, s32[16,256]{1,0:T(8,128)} %m_in.1, f32[128,128]{1,0:T(8,128)} %maximum_convert_fusion.norms, bf16[32,128,512]{2,1,0:T(8,128)(2,1)} %bitcast.7, bf16[32,128,128]{2,1,0:T(8,128)(2,1)} %bitcast.10, bf16[32,128,128]{2,1,0:T(8,128)(2,1)} %bitcast.11), custom_call_target="tpu_custom_call" | custom-call | tf_op jit(solution)/shard_map/pallas_call | solution.py:490
  1128.1 2.3 copy.9
